TPU v7x, 128 devices: a whole 4x4x4 slice. The times are simulated.
128 devices in a mesh: tp: 4 (over x), sp: 32 (over z, y, core).
Axes of the slice: x: 4, y: 4, z: 4, core: 2. Of those that a mesh axis runs over, the one named last changes fastest.
Arguments:
- x: bfloat16 [8, 4096], replicated
- seq_len: int32 [8], replicated
- ln_w: bfloat16 [4096], replicated
- w_q: bfloat16 [4096, 4096], P(None, 'tp')
- w_o: bfloat16 [4096, 4096], P('tp')
- w_gate: bfloat16 [4096, 14336], P(None, 'tp')
- w_up: bfloat16 [4096, 14336], P(None, 'tp')
- w_down: bfloat16 [14336, 4096], P('tp')
- k_cache: bfloat16 [8, 8, 32768, 128], P(None, 'tp', 'sp')
- v_cache: bfloat16 [8, 8, 32768, 128], P(None, 'tp', 'sp')
Outputs:
- output: bfloat16 [8, 4096], replicated
All inputs are finite; a program needn't handle non-finite values.
Results may differ from a plain program's by a relative error of at most 0.00718116.
Values sent between devices are 32-bit elements.
A program may use at most 1 GiB of HBM per device.

v0:
```python
import jax
import jax.numpy as jnp
from jax import lax
from jax.sharding import PartitionSpec as P

LN_EPS = 1e-5
NEG_BIG = -1e30


def layer_norm(x, ln_w):
    x_f32 = x.astype(jnp.float32)
    centered = x_f32 - jnp.mean(x_f32, axis=-1, keepdims=True)
    variance = jnp.mean(centered * centered, axis=-1, keepdims=True)
    return (centered * lax.rsqrt(variance + LN_EPS) * ln_w.astype(jnp.float32)).astype(jnp.bfloat16)


def project(act_in, weight):
    return jnp.dot(act_in, weight, preferred_element_type=jnp.float32)


def solution(mesh):
    cache_spec = P(None, 'tp', 'sp', None)
    col_spec = P(None, 'tp')
    row_spec = P('tp', None)

    def local_step(x, seq_len, ln_w, w_q, w_o, w_gate, w_up, w_down, k_cache, v_cache):
        n_rows, kv_local, seq_block, head_dim = k_cache.shape
        heads_local = w_q.shape[1] // head_dim
        group_size = heads_local // kv_local
        hidden = layer_norm(x, ln_w)
        query = project(hidden, w_q).astype(jnp.bfloat16).reshape(n_rows, kv_local, group_size, head_dim)
        positions = lax.axis_index('sp') * seq_block + jnp.arange(seq_block)
        is_live = (positions[None, :] <= seq_len[:, None])[:, None, None, :]
        scores = jnp.einsum('bkgd,bksd->bkgs', query, k_cache, preferred_element_type=jnp.float32) * head_dim ** -0.5
        scores = jnp.where(is_live, scores, NEG_BIG)
        block_max = jnp.max(scores, axis=-1)
        probs = jnp.where(is_live, jnp.exp(scores - block_max[..., None]), 0.0)
        block_sum = jnp.sum(probs, axis=-1)
        block_out = jnp.einsum('bkgs,bksd->bkgd', probs.astype(jnp.bfloat16), v_cache, preferred_element_type=jnp.float32)
        all_out = lax.all_gather(block_out, 'sp')
        all_max = lax.all_gather(block_max, 'sp')
        all_sum = lax.all_gather(block_sum, 'sp')
        glob_max = jnp.max(all_max, axis=0)
        rescale = jnp.exp(all_max - glob_max)
        total_sum = jnp.sum(all_sum * rescale, axis=0)
        attn_vals = jnp.sum(all_out * rescale[..., None], axis=0) / total_sum[..., None]
        attn_vals = attn_vals.reshape(n_rows, heads_local * head_dim).astype(jnp.bfloat16)
        attn_proj = lax.psum(project(attn_vals, w_o), 'tp')
        act_vals = (jax.nn.silu(project(hidden, w_gate)) * project(hidden, w_up)).astype(jnp.bfloat16)
        mlp_proj = lax.psum(project(act_vals, w_down), 'tp')
        x_out = (x.astype(jnp.float32) + attn_proj + mlp_proj).astype(jnp.bfloat16)
        return x_out

    return jax.shard_map(local_step, mesh=mesh,
                         in_specs=(P(), P(), P(), col_spec, row_spec,
                                   col_spec, col_spec, row_spec, cache_spec, cache_spec),
                         out_specs=P(), check_vma=False)
```

profile of v0, /device:TPU:1, one launch (start us, length us, event | category | flops | bytes accessed | tf_op | source)
XLA Modules:
  0.0 157.5 jit_solution(10287426568375911936)
XLA Ops:
  6.5 0.0 all-gather.5.cloned.1.call-start
  6.5 1.0 convert_reduce_fusion
  7.5 1.1 fusion.7
  8.6 0.7 convert_element_type.29
  9.3 0.9 broadcast_compare_fusion
  10.2 5.0 %convolution_convert_fusion = bf16[8,1024]{1,0:T(8,128)(2,1)S(1)} fusion(bf16[4096,1024]{1,0:T(8,128)(2,1)} %param.13, bf16[8,4096]{1,0:T(8,128)(2,1)} %param.10, f32[4096]{0:T(1024)S(1)} %convert_element_type.29, f32[8]{0:T(128)S(1)} %add_rsqrt_fusion, f32[8]{0:T(128)S(1)} %broadcast_multiply_fusion), kind=kOutput, calls=%fused_computation.5 | convolution fusion | flops 67280896 | bytes 8486976 | tf_op jit(solution)/shard_map/dot_general | solution.py:18
  15.2 1.3 fusion.31
  16.5 1.4 fusion.10
  17.9 0.0 all-gather.5.cloned.1.call-update
  17.9 0.0 all-reduce.3.cloned.1.call-start
  17.9 27.5 %all-gather.1 = f32[256,2,4]{2,1,0:T(2,128)S(1)} all-gather(f32[8,2,4]{2,1,0:T(2,128)S(1)} %get-tuple-element.7), channel_id=3, replica_groups=mesh['tp'=4,'sp'=32] {'sp'}, dimensions={0}, use_global_device_ids=true | all-gather | bytes 8448 | tf_op jit(solution)/shard_map/all_gather | solution.py:41
  45.5 0.3 fusion.3
  45.8 0.1 reduce_max.19
  45.9 0.2 subtract_exponential_fusion
  46.0 24.3 %all-gather.2 = f32[256,2,4]{2,1,0:T(2,128)S(1)} all-gather(f32[8,2,4]{2,1,0:T(2,128)S(1)} %fusion.3), channel_id=4, replica_groups=mesh['tp'=4,'sp'=32] {'sp'}, dimensions={0}, use_global_device_ids=true | all-gather | bytes 8448 | tf_op jit(solution)/shard_map/all_gather | solution.py:42
  70.4 11.4 %fusion.28 = f32[8,3584]{1,0:T(8,128)S(1)} fusion(bf16[4096,3584]{1,0:T(8,128)(2,1)} %param.15, bf16[8,4096]{1,0:T(8,128)(2,1)S(1)} %copy-done, f32[4096]{0:T(1024)S(1)} %convert_element_type.29, f32[8]{0:T(128)S(1)} %add_rsqrt_fusion, f32[8]{0:T(128)S(1)} %broadcast_multiply_fusion), kind=kOutput, calls=%fused_computation.40 | convolution fusion | flops 235044864 | bytes 29556800 | tf_op jit(solution)/shard_map/dot_general | solution.py:18
  81.8 0.2 multiply_reduce_fusion.1
  82.0 22.1 %fusion.1 = f32[8,4096]{1,0:T(8,128)} fusion(bf16[3584,4096]{1,0:T(8,128)(2,1)} %param.17, bf16[4096,3584]{1,0:T(8,128)(2,1)} %param.16, f32[8,3584]{1,0:T(8,128)S(1)} %fusion.28, bf16[8,4096]{1,0:T(8,128)(2,1)S(1)} %copy-done, f32[4096]{0:T(1024)S(1)} %convert_element_type.29, f32[8]{0:T(128)S(1)} %add_rsqrt_fusion, f32[8]{0:T(128)S(1)} %broadcast_multiply_fusion), kind=kOutput, calls=%fused_computation.2 | convolution fusion | flops 470097920 | bytes 59048000 | tf_op jit(solution)/shard_map/dot_general | solution.py:18
  104.2 1.8 %multiply_reduce_fusion = f32[8,2,4,128]{3,2,1,0:T(4,128)S(1)} fusion(f32[32,8,2,4,128]{4,3,2,1,0:T(4,128)} %bitcast.14, f32[32,8,2,4]{3,2,1,0:T(2,128)S(1)} %subtract_exponential_fusion), kind=kLoop, calls=%fused_computation.6 | loop fusion | flops 516096 | bytes 1089536 | tf_op jit(solution)/shard_map/reduce_sum | solution.py:46
  105.9 0.1 divide_convert_fusion
  106.0 5.2 %fusion.32 = f32[8,4096]{1,0:T(8,128)} fusion(bf16[8,1024]{1,0:T(8,128)(2,1)S(1)} %convert_element_type.34, bf16[1024,4096]{1,0:T(8,128)(2,1)} %param.14), kind=kOutput, calls=%fused_computation.42 | convolution fusion | flops 67108864 | bytes 8536064 | tf_op jit(solution)/shard_map/dot_general | solution.py:18
  111.3 0.0 all-reduce.3.cloned.1.call-update
  111.3 37.7 %all-reduce.3.cloned.1.call-done = (f32[8,4096]{1,0:T(8,128)}, f32[8,4096]{1,0:T(8,128)}) async-done(((f32[8,4096]{1,0:T(8,128)}, f32[8,4096]{1,0:T(8,128)}), (f32[8,4096]{1,0:T(8,128)}, f32[8,4096]{1,0:T(8,128)})) %all-reduce.3.cloned.1.call-update) | async-done | bytes 262160 | tf_op jit(solution)/shard_map/psum | solution.py:50
  149.0 1.6 %fusion.13 = bf16[8,4096]{1,0:T(8,128)(2,1)} fusion(f32[8,4096]{1,0:T(8,128)} %get-tuple-element.5, f32[8,4096]{1,0:T(8,128)} %get-tuple-element.6, bf16[8,4096]{1,0:T(8,128)(2,1)S(1)} %copy-done), kind=kLoop, calls=%fused_computation.22 | loop fusion | flops 131072 | bytes 393216 | tf_op jit(solution)/shard_map/convert_element_type | solution.py:51
  (11 shorter events, 0.0 us)
Async XLA Ops:
  6.5 97.6 %all-gather.5.cloned.1.call-start = ((), (), s32[]{:S(2)}) async-start(), calls=%async_computation | async-start | bytes 1081344 | tf_op jit(solution)/shard_map/all_gather | solution.py:40
  9.3 5.9 %copy-start.1 = (bf16[8,2,1024,128]{3,2,1,0:T(8,128)(2,1)S(1)}, bf16[8,2,1024,128]{3,2,1,0:T(8,128)(2,1)}, u32[]{:S(2)}) copy-start(bf16[8,2,1024,128]{3,2,1,0:T(8,128)(2,1)} %param.18) | copy-start | bytes 12582916
  10.2 6.3 %copy-start.2 = (bf16[8,2,1024,128]{3,2,1,0:T(8,128)(2,1)S(1)}, bf16[8,2,1024,128]{3,2,1,0:T(8,128)(2,1)}, u32[]{:S(2)}) copy-start(bf16[8,2,1024,128]{3,2,1,0:T(8,128)(2,1)} %param.19) | copy-start | bytes 12582916
  15.2 55.2 %copy-start = (bf16[8,4096]{1,0:T(8,128)(2,1)S(1)}, bf16[8,4096]{1,0:T(8,128)(2,1)}, u32[]{:S(2)}) copy-start(bf16[8,4096]{1,0:T(8,128)(2,1)} %param.10) | copy-start | bytes 196612
  17.9 131.1 %all-reduce.3.cloned.1.call-start = ((), (), s32[]{:S(2)}) async-start(), calls=%async_computation.1 | async-start | bytes 524288 | tf_op jit(solution)/shard_map/psum | solution.py:50
Sparse Core Ops, SparseCore 0:
  18.0 46.3 all-gather.4
  111.4 37.5 all-reduce.2
where the time goes:
time: 159 us; the launch traced here: 157 us
  blocking collectives  51.9 us (33%)
  matrix products  46.4 us (29%)
  waiting for transfers between devices  37.7 us (24%)
  between operations  13.4 us (8%)
  other arithmetic  7.91 us (5%)
    dot_general x4, matrix products, project(): return jnp.dot(act_in, weight, preferred_element_type=jnp.float32)  43.8 us
    psum x1, waiting for transfers between devices, local_step(): mlp_proj = lax.psum(project(act_vals, w_down), 'tp')  37.7 us
    all_gather x1, blocking collectives, local_step(): all_max = lax.all_gather(block_max, 'sp')  27.5 us
    all_gather x1, blocking collectives, local_step(): all_sum = lax.all_gather(block_sum, 'sp')  24.3 us
  transfers between devices with their start and end apart: 2, of which 1 were waited for; matrix products, arithmetic and copies ran while one was open for 22% of the time, Pallas kernels for 0%

commit v1 on v0

v1 whole, which is shorter than its diff:
```python
import functools

import jax
import jax.numpy as jnp
from jax import lax
from jax.experimental import pallas as pl
from jax.experimental.pallas import tpu as pltpu
from jax.sharding import PartitionSpec as P

LN_EPS = 1e-5
NEG_BIG = -1e30
LOG2E = 1.4426950408889634
MESH = pl.DeviceIdType.MESH
F32 = jnp.float32
BF16 = jnp.bfloat16

ROWS = 8
HID = 4096
HD = 128
BLK = 1024
FF_BLOCKS = 28
WQ_CHUNKS = 4


def kernel(x_hbm, len_hbm, lnw_hbm, wq_hbm, wo_hbm, wg_hbm, wu_hbm, wd_hbm, k_hbm, v_hbm, out_ref,
           x_v, lnw_v, len_s, wq_v, wg_v, wu_v, k_v, v_v, wo_v, wd_v,
           q_b, mz_b, mg_b, ds_b, dr_b, y_b, z_b, of_b, xs_b, g_b,
           in_sem, wq_sem, gu_sem, k_sem, v_sem, w2_sem,
           q_ss, q_rs, mz_ss, mz_rs, mg_ss, mg_rs, d_ss, d_rs, y_ss, y_rs, z_ss, z_rs, x_ss, x_rs, g_ss, g_rs):
    xi = lax.axis_index('tp')
    sp = lax.axis_index('sp')
    c = lax.rem(sp, 2)
    y = lax.rem(lax.div(sp, 2), 4)
    z = lax.div(sp, 8)
    oc = 1 - c
    grp = y * 2 + c

    def dev(x_, z_, y_, c_):
        return (x_, (z_ * 4 + y_) * 2 + c_)

    def up(v, k):
        return lax.rem(v + k, 4)

    partner = dev(xi, z, y, oc)
    z_peers = [dev(xi, up(z, k), y, c) for k in (1, 2, 3)]
    y_peers = [dev(xi, z, up(y, k), c) for k in (1, 2, 3)]
    x_peers = [dev(up(xi, k), z, y, c) for k in (1, 2, 3)]
    yo_peers = [dev(xi, z, up(y, k), oc) for k in (1, 2, 3)]

    bar = pltpu.get_barrier_semaphore()
    everyone = [partner] + z_peers + y_peers + x_peers + yo_peers
    for d in everyone:
        pl.semaphore_signal(bar, inc=1, device_id=d, device_id_type=MESH)

    def start(src, dst, sem):
        cp = pltpu.make_async_copy(src, dst, sem)
        cp.start()
        return cp

    cp_x = start(x_hbm, x_v, in_sem.at[0])
    cp_lnw = start(lnw_hbm, lnw_v, in_sem.at[1])
    cp_len = start(len_hbm, len_s, in_sem.at[2])
    kc = HID // WQ_CHUNKS
    cp_wq = [start(wq_hbm.at[pl.ds(i * kc, kc), pl.ds(pl.multiple_of(c * 512, 512), 512)], wq_v.at[i], wq_sem.at[i])
             for i in range(WQ_CHUNKS)]
    ff = pl.multiple_of(jnp.minimum(z * 8 + grp, FF_BLOCKS - 1) * 128, 128)
    cp_g = start(wg_hbm.at[:, pl.ds(ff, 128)], wg_v, gu_sem.at[0])
    cp_u = start(wu_hbm.at[:, pl.ds(ff, 128)], wu_v, gu_sem.at[1])

    def row_of(j):
        return 4 * oc + j if j < 4 else 4 * c + (j - 4)

    cp_k, cp_v = [], []
    for j in range(8):
        cp_k.append(start(k_hbm.at[row_of(j)], k_v.at[j], k_sem.at[j]))
        cp_v.append(start(v_hbm.at[row_of(j)], v_v.at[j], v_sem.at[j]))
    cols = pl.ds(pl.multiple_of(y * 1024, 1024), 1024)
    cp_wo = start(wo_hbm.at[:, cols], wo_v, w2_sem.at[0])
    cp_wd = start(wd_hbm.at[:, cols], wd_v, w2_sem.at[1])

    sends = []

    def send(src, dst, ss, rs, d):
        cp = pltpu.make_async_remote_copy(src_ref=src, dst_ref=dst, send_sem=ss, recv_sem=rs,
                                          device_id=d, device_id_type=MESH)
        cp.start()
        sends.append(cp)

    def recv(dst, ss, rs, d):
        pltpu.make_async_remote_copy(src_ref=dst, dst_ref=dst, send_sem=ss, recv_sem=rs,
                                     device_id=d, device_id_type=MESH).wait_recv()

    cp_x.wait()
    cp_lnw.wait()
    xf = x_v[...].astype(F32)
    cen = xf - jnp.mean(xf, axis=-1, keepdims=True)
    var = jnp.mean(cen * cen, axis=-1, keepdims=True)
    h = (cen * lax.rsqrt(var + LN_EPS) * lnw_v[...].astype(F32).reshape(1, HID)).astype(BF16)

    q = jnp.zeros((ROWS, 512), F32)
    for i in range(WQ_CHUNKS):
        cp_wq[i].wait()
        q = q + jnp.dot(h[:, i * kc:(i + 1) * kc], wq_v[i], preferred_element_type=F32)
    q = q.astype(BF16).astype(F32)
    qrows = pl.ds(pl.multiple_of(c * 32, 32), 32)
    q_b[qrows, :] = jnp.concatenate([q[:, i * HD:(i + 1) * HD] for i in range(4)], axis=0)
    pl.semaphore_wait(bar, len(everyone))
    send(q_b.at[qrows, :], q_b.at[qrows, :], q_ss.at[0], q_rs.at[0], partner)

    cp_g.wait()
    cp_u.wait()
    gu = jnp.dot(h, jnp.concatenate([wg_v[...], wu_v[...]], axis=1), preferred_element_type=F32)
    act = (jax.nn.silu(gu[:, :HD]) * gu[:, HD:]).astype(BF16).astype(F32)
    mz_b[z] = act
    for k in (1, 2, 3):
        send(mz_b.at[z], mz_b.at[z], mz_ss.at[k - 1], mz_rs.at[z], z_peers[k - 1])

    prow = pl.ds(pl.multiple_of(oc * 32, 32), 32)
    recv(q_b.at[prow, :], q_ss.at[0], q_rs.at[0], partner)
    cp_len.wait()
    lane = lax.broadcasted_iota(jnp.int32, (ROWS, HD), 1)
    top = lax.broadcasted_iota(jnp.int32, (ROWS, HD), 0) < 4
    pos = sp * BLK + lax.broadcasted_iota(jnp.int32, (ROWS, BLK), 1)
    cs = (HD ** -0.5) * LOG2E

    def attend(j):
        b = row_of(j)
        qh = q_b[pl.ds(b, 8, stride=8), :]
        qd = jnp.concatenate([jnp.where(top, qh, 0.0), jnp.where(top, 0.0, qh)], axis=1).astype(BF16)
        cp_k[j].wait()
        kk = jnp.concatenate([k_v[j, 0], k_v[j, 1]], axis=1)
        s = lax.dot_general(qd, kk, (((1,), (1,)), ((), ())), preferred_element_type=F32)
        s = jnp.where(pos <= len_s[b], s, -jnp.inf)
        m = jnp.maximum(jnp.max(s, axis=-1, keepdims=True), NEG_BIG)
        p = jnp.exp2((s - m) * cs)
        l = jnp.sum(p, axis=-1, keepdims=True)
        cp_v[j].wait()
        vv = jnp.concatenate([v_v[j, 0], v_v[j, 1]], axis=1)
        o2 = jnp.dot(p.astype(BF16), vv, preferred_element_type=F32)
        return jnp.where(top, o2[:, :HD], o2[:, HD:]), m, l

    def stats_tile(ms, ls):
        t = jnp.zeros((ROWS, HD), F32)
        for i in range(4):
            t = jnp.where(lane == i, ms[i], t)
            t = jnp.where(lane == 4 + i, ls[i], t)
        return t

    ms, ls = [], []
    for j in range(4):
        o, m, l = attend(j)
        ds_b[j] = o
        ms.append(m)
        ls.append(l)
    ds_b[4] = stats_tile(ms, ls)
    send(ds_b, dr_b, d_ss.at[0], d_rs.at[0], partner)
    own = [attend(j) for j in range(4, 8)]

    def combine(parts):
        mx = functools.reduce(jnp.maximum, [p[1] for p in parts])
        ws = [jnp.exp2((p[1] - mx) * cs) for p in parts]
        o = functools.reduce(jnp.add, [p[0] * w for p, w in zip(parts, ws)])
        l = functools.reduce(jnp.add, [p[2] * w for p, w in zip(parts, ws)])
        return o, mx, l

    def unpack(tile_of, i, st):
        return tile_of(i), st[:, i:i + 1], st[:, 4 + i:5 + i]

    recv(dr_b, d_ss.at[0], d_rs.at[0], partner)
    st = dr_b[4]
    ms, ls = [], []
    for i in range(4):
        o, m, l = combine([own[i], unpack(lambda r: dr_b[r], i, st)])
        y_b[y, i] = o
        ms.append(m)
        ls.append(l)
    y_b[y, 4] = stats_tile(ms, ls)
    for k in (1, 2, 3):
        send(y_b.at[y], y_b.at[y], y_ss.at[k - 1], y_rs.at[y], y_peers[k - 1])

    for k in (1, 2, 3):
        recv(mz_b.at[up(z, k)], mz_ss.at[k - 1], mz_rs.at[up(z, k)], z_peers[k - 1])
    mg_b[grp] = mz_b[...]
    gpeers = ([(partner, y * 2 + oc)] + [(y_peers[k - 1], up(y, k) * 2 + c) for k in (1, 2, 3)]
              + [(yo_peers[k - 1], up(y, k) * 2 + oc) for k in (1, 2, 3)])
    for n, (d, _) in enumerate(gpeers):
        send(mz_b, mg_b.at[grp], mg_ss.at[n], mg_rs.at[grp], d)

    for k in (1, 2, 3):
        recv(y_b.at[up(y, k)], y_ss.at[k - 1], y_rs.at[up(y, k)], y_peers[k - 1])
    ms, ls = [], []
    sts = [y_b[n, 4] for n in range(4)]
    for i in range(4):
        o, m, l = combine([unpack(lambda r, n=n: y_b[n, r], i, sts[n]) for n in range(4)])
        z_b[z, i] = o
        ms.append(m)
        ls.append(l)
    z_b[z, 4] = stats_tile(ms, ls)
    for k in (1, 2, 3):
        send(z_b.at[z], z_b.at[z], z_ss.at[k - 1], z_rs.at[z], z_peers[k - 1])

    for n, (d, g) in enumerate(gpeers):
        recv(mg_b.at[g], mg_ss.at[n], mg_rs.at[g], d)
    ml = jnp.concatenate([mg_b[i % 8, i // 8] for i in range(FF_BLOCKS)], axis=1).astype(BF16)
    cp_wd.wait()
    r1 = jnp.dot(ml, wd_v[:, :512], preferred_element_type=F32)
    r2 = jnp.dot(ml, wd_v[:, 512:], preferred_element_type=F32)

    for k in (1, 2, 3):
        recv(z_b.at[up(z, k)], z_ss.at[k - 1], z_rs.at[up(z, k)], z_peers[k - 1])
    sts = [z_b[n, 4] for n in range(4)]
    for i in range(4):
        o, m, l = combine([unpack(lambda r, n=n: z_b[n, r], i, sts[n]) for n in range(4)])
        o = o / l
        of_b[pl.ds(i * 8, 8), :] = o
        of_b[pl.ds(32 + i * 8, 8), :] = o
    ol = jnp.concatenate([of_b[pl.ds(n, 8, stride=8), :] for n in range(8)], axis=1).astype(BF16)
    cp_wo.wait()
    r1 = r1 + jnp.dot(ol, wo_v[:, :512], preferred_element_type=F32)
    r2 = r2 + jnp.dot(ol, wo_v[:, 512:], preferred_element_type=F32)

    upper = lax.broadcasted_iota(jnp.int32, (ROWS, 512), 0) < 4
    keep = jnp.logical_xor(upper, jnp.broadcast_to(c == 1, (ROWS, 512)))
    xs_b[xi] = jnp.where(keep, r1, pltpu.roll(r2, 4, 0))
    for k in (1, 2, 3):
        send(xs_b.at[xi], xs_b.at[xi], x_ss.at[k - 1], x_rs.at[xi], x_peers[k - 1])
    xc = x_v[:, pl.ds(pl.multiple_of(y * 1024, 1024), 1024)].astype(F32)
    xr = jnp.where(keep, xc[:, :512], pltpu.roll(xc[:, 512:], 4, 0))
    for k in (1, 2, 3):
        recv(xs_b.at[up(xi, k)], x_ss.at[k - 1], x_rs.at[up(xi, k)], x_peers[k - 1])
    tot = xr + ((xs_b[0] + xs_b[1]) + (xs_b[2] + xs_b[3]))
    g_b[grp] = tot.astype(BF16).astype(F32)
    for n, (d, _) in enumerate(gpeers):
        send(g_b.at[grp], g_b.at[grp], g_ss.at[n], g_rs.at[grp], d)
    for n, (d, g) in enumerate(gpeers):
        recv(g_b.at[g], g_ss.at[n], g_rs.at[g], d)
    for yy in range(4):
        a0, a1 = g_b[2 * yy], g_b[2 * yy + 1]
        out_ref[:, yy * 1024:yy * 1024 + 512] = jnp.where(upper, a0, a1).astype(BF16)
        out_ref[:, yy * 1024 + 512:yy * 1024 + 1024] = pltpu.roll(jnp.where(upper, a1, a0), 4, 0).astype(BF16)
    for cp in sends:
        cp.wait_send()


def solution(mesh):
    cache_spec = P(None, 'tp', 'sp', None)
    col_spec = P(None, 'tp')
    row_spec = P('tp', None)
    any_spec = pl.BlockSpec(memory_space=pl.ANY)
    dma = pltpu.SemaphoreType.DMA

    def local_step(*args):
        return pl.pallas_call(
            kernel,
            out_shape=jax.ShapeDtypeStruct((ROWS, HID), BF16),
            in_specs=[any_spec] * 10,
            out_specs=pl.BlockSpec(memory_space=pltpu.VMEM),
            scratch_shapes=[
                pltpu.VMEM((ROWS, HID), BF16),
                pltpu.VMEM((HID,), BF16),
                pltpu.SMEM((ROWS,), jnp.int32),
                pltpu.VMEM((WQ_CHUNKS, HID // WQ_CHUNKS, 512), BF16),
                pltpu.VMEM((HID, HD), BF16),
                pltpu.VMEM((HID, HD), BF16),
                pltpu.VMEM((8, 2, BLK, HD), BF16),
                pltpu.VMEM((8, 2, BLK, HD), BF16),
                pltpu.VMEM((1024, 1024), BF16),
                pltpu.VMEM((3584, 1024), BF16),
                pltpu.VMEM((64, HD), F32),
                pltpu.VMEM((4, ROWS, HD), F32),
                pltpu.VMEM((8, 4, ROWS, HD), F32),
                pltpu.VMEM((5, ROWS, HD), F32),
                pltpu.VMEM((5, ROWS, HD), F32),
                pltpu.VMEM((4, 5, ROWS, HD), F32),
                pltpu.VMEM((4, 5, ROWS, HD), F32),
                pltpu.VMEM((64, HD), F32),
                pltpu.VMEM((4, ROWS, 512), F32),
                pltpu.VMEM((8, ROWS, 512), F32),
                dma((3,)), dma((WQ_CHUNKS,)), dma((2,)), dma((8,)), dma((8,)), dma((2,)),
                dma((1,)), dma((1,)),
                dma((3,)), dma((4,)),
                dma((7,)), dma((8,)),
                dma((1,)), dma((1,)),
                dma((3,)), dma((4,)),
                dma((3,)), dma((4,)),
                dma((3,)), dma((4,)),
                dma((7,)), dma((8,)),
            ],
            compiler_params=pltpu.CompilerParams(collective_id=0, has_side_effects=True,
                                                 vmem_limit_bytes=56 * 1024 * 1024),
        )(*args)

    return jax.shard_map(local_step, mesh=mesh,
                         in_specs=(P(), P(), P(), col_spec, row_spec,
                                   col_spec, col_spec, row_spec, cache_spec, cache_spec),
                         out_specs=P(), check_vma=False)
```

time: 159 us -> 38.3 us (0.24)
  blocking collectives: 51.9 us -> 0 us
  matrix products: 46.4 us -> 0 us
  waiting for transfers between devices: 37.7 us -> 0 us
  Pallas kernels: 0 us -> 36.7 us
  between operations: 13.4 us -> 0.01 us
  other arithmetic: 7.91 us -> 0 us
    all_gather x2 -> x0, blocking collectives: 51.9 us -> none  [the longest x1 27.5 us: local_step(): all_max = lax.all_gather(block_max, 'sp')]
    dot_general x6 -> x0, matrix products: 46.4 us -> none  [the longest x4 43.8 us: project(): return jnp.dot(act_in, weight, preferred_element_type=jnp.float32)]
    psum x1 -> x0, waiting for transfers between devices: 37.7 us -> none  [local_step(): mlp_proj = lax.psum(project(act_vals, w_down), 'tp')]
    pallas_call x0 -> x1, Pallas kernels: none -> 36.7 us  [local_step(): pl.pallas_call(kernel, out_shape=jax.ShapeDtypeStruct((ROWS, HID), BF16),...]
    reduce_sum x5 -> x0, other arithmetic: 4.31 us -> none  [the longest x1 1.76 us: local_step(): jnp.sum(all_out * rescale[..., None], axis=0) / total_sum[..., None]]
    convert_element_type x3 -> x0, other arithmetic: 2.41 us -> none  [the longest x1 1.61 us: local_step(): x_out = (x.astype(jnp.float32) + attn_proj + mlp_proj).astype(jnp.bfloat16)]
  transfers between devices with their start and end apart: 2 -> 0, of which waited for: 1 -> 0; matrix products, arithmetic and copies ran while one was open for 22% -> 0% of each run, Pallas kernels for 0% -> 0%
where the time goes in v1:
time: 38.3 us; the launch traced here: 38.1 us
  Pallas kernels  36.7 us (96%)
  local copies, waits for them, and re-layouts  1.47 us (4%)
    pallas_call x1, Pallas kernels, local_step(): pl.pallas_call(kernel, out_shape=jax.ShapeDtypeStruct((ROWS, HID), BF16),...  36.7 us
    unnamed x1, local copies, waits for them, and re-layouts  1.47 us

profile of v1, /device:TPU:1, one launch (start us, length us, event | category | flops | bytes accessed | tf_op | source)
XLA Modules:
  0.0 38.1 jit_solution(7122537755077675875)
XLA Ops:
  0.0 36.7 %shard_map.100 = bf16[8,4096]{1,0:T(8,128)(2,1)} custom-call(bf16[8,4096]{1,0:T(8,128)(2,1)} %x_hbm.1, s32[8]{0:T(128)} %len_hbm.1, bf16[4096]{0:T(1024)(128)(2,1)} %lnw_hbm.1, bf16[4096,1024]{1,0:T(8,128)(2,1)} %wq_hbm.1, bf16[1024,4096]{1,0:T(8,128)(2,1)} %wo_hbm.1, bf16[4096,3584]{1,0:T(8,128)(2,1)} %wg_hbm.1, bf16[4096,3584]{1,0:T(8,128)(2,1)} %wu_hbm.1, ...), custom_call_target="tpu_custom_call" | custom-call | tf_op jit(solution)/shard_map/pallas_call | solution.py:253
  36.7 1.5 %copy.12 = bf16[8,4096]{1,0:T(8,128)(2,1)} copy(bf16[8,4096]{1,0:T(8,128)(2,1)} %shard_map.100) | data formatting | bytes 131072

commit v2 on v1

--- a/solution.py
+++ b/solution.py
@@ -24,7 +24,7 @@
 
 def kernel(x_hbm, len_hbm, lnw_hbm, wq_hbm, wo_hbm, wg_hbm, wu_hbm, wd_hbm, k_hbm, v_hbm, out_ref,
            x_v, lnw_v, len_s, wq_v, wg_v, wu_v, k_v, v_v, wo_v, wd_v,
-           q_b, mz_b, mg_b, ds_b, dr_b, y_b, z_b, of_b, xs_b, g_b,
+           q_b, mz_b, mg_b, ds_b, dr_b, y_b, z_b, of_b, f_b, xs_b, g_b,
            in_sem, wq_sem, gu_sem, k_sem, v_sem, w2_sem,
            q_ss, q_rs, mz_ss, mz_rs, mg_ss, mg_rs, d_ss, d_rs, y_ss, y_rs, z_ss, z_rs, x_ss, x_rs, g_ss, g_rs):
     xi = lax.axis_index('tp')
@@ -47,36 +47,41 @@
     x_peers = [dev(up(xi, k), z, y, c) for k in (1, 2, 3)]
     yo_peers = [dev(xi, z, up(y, k), oc) for k in (1, 2, 3)]
 
+    def start(src, dst, sem):
+        cp = pltpu.make_async_copy(src, dst, sem)
+        cp.start()
+        return cp
+
+    cp_x = start(x_hbm, x_v, in_sem.at[0])
+    cp_lnw = start(lnw_hbm, lnw_v, in_sem.at[1])
+    kc = HID // WQ_CHUNKS
+    cp_wq = [start(wq_hbm.at[pl.ds(i * kc, kc), pl.ds(pl.multiple_of(c * 512, 512), 512)], wq_v.at[i], wq_sem.at[i])
+             for i in range(WQ_CHUNKS)]
+
     bar = pltpu.get_barrier_semaphore()
     everyone = [partner] + z_peers + y_peers + x_peers + yo_peers
     for d in everyone:
         pl.semaphore_signal(bar, inc=1, device_id=d, device_id_type=MESH)
 
-    def start(src, dst, sem):
-        cp = pltpu.make_async_copy(src, dst, sem)
-        cp.start()
-        return cp
-
-    cp_x = start(x_hbm, x_v, in_sem.at[0])
-    cp_lnw = start(lnw_hbm, lnw_v, in_sem.at[1])
-    cp_len = start(len_hbm, len_s, in_sem.at[2])
-    kc = HID // WQ_CHUNKS
-    cp_wq = [start(wq_hbm.at[pl.ds(i * kc, kc), pl.ds(pl.multiple_of(c * 512, 512), 512)], wq_v.at[i], wq_sem.at[i])
-             for i in range(WQ_CHUNKS)]
     ff = pl.multiple_of(jnp.minimum(z * 8 + grp, FF_BLOCKS - 1) * 128, 128)
     cp_g = start(wg_hbm.at[:, pl.ds(ff, 128)], wg_v, gu_sem.at[0])
     cp_u = start(wu_hbm.at[:, pl.ds(ff, 128)], wu_v, gu_sem.at[1])
+    cp_len = start(len_hbm, len_s, in_sem.at[2])
 
     def row_of(j):
-        return 4 * oc + j if j < 4 else 4 * c + (j - 4)
-
-    cp_k, cp_v = [], []
-    for j in range(8):
-        cp_k.append(start(k_hbm.at[row_of(j)], k_v.at[j], k_sem.at[j]))
-        cp_v.append(start(v_hbm.at[row_of(j)], v_v.at[j], v_sem.at[j]))
+        return lax.rem(4 * oc + j, 8)
+
+    def kv_copies(j):
+        return (pltpu.make_async_copy(k_hbm.at[row_of(j)], k_v.at[j], k_sem.at[j]),
+                pltpu.make_async_copy(v_hbm.at[row_of(j)], v_v.at[j], v_sem.at[j]))
+
+    @pl.loop(0, 8)
+    def _(j):
+        for cp in kv_copies(j):
+            cp.start()
+
     cols = pl.ds(pl.multiple_of(y * 1024, 1024), 1024)
-    cp_wo = start(wo_hbm.at[:, cols], wo_v, w2_sem.at[0])
-    cp_wd = start(wd_hbm.at[:, cols], wd_v, w2_sem.at[1])
+    cp_k, cp_v = zip(*[kv_copies(j) for j in range(8)])
 
     sends = []
 
@@ -123,21 +128,28 @@
     pos = sp * BLK + lax.broadcasted_iota(jnp.int32, (ROWS, BLK), 1)
     cs = (HD ** -0.5) * LOG2E
 
-    def attend(j):
-        b = row_of(j)
-        qh = q_b[pl.ds(b, 8, stride=8), :]
-        qd = jnp.concatenate([jnp.where(top, qh, 0.0), jnp.where(top, 0.0, qh)], axis=1).astype(BF16)
-        cp_k[j].wait()
-        kk = jnp.concatenate([k_v[j, 0], k_v[j, 1]], axis=1)
-        s = lax.dot_general(qd, kk, (((1,), (1,)), ((), ())), preferred_element_type=F32)
-        s = jnp.where(pos <= len_s[b], s, -jnp.inf)
-        m = jnp.maximum(jnp.max(s, axis=-1, keepdims=True), NEG_BIG)
-        p = jnp.exp2((s - m) * cs)
-        l = jnp.sum(p, axis=-1, keepdims=True)
-        cp_v[j].wait()
-        vv = jnp.concatenate([v_v[j, 0], v_v[j, 1]], axis=1)
-        o2 = jnp.dot(p.astype(BF16), vv, preferred_element_type=F32)
-        return jnp.where(top, o2[:, :HD], o2[:, HD:]), m, l
+    def attend(js):
+        for j in js:
+            cp_k[j].wait()
+        for j in js:
+            cp_v[j].wait()
+        ss = []
+        for j in js:
+            b = row_of(j)
+            qh = q_b[pl.ds(b, 8, stride=8), :]
+            qd = jnp.concatenate([jnp.where(top, qh, 0.0), jnp.where(top, 0.0, qh)], axis=1).astype(BF16)
+            kk = jnp.concatenate([k_v[j, 0], k_v[j, 1]], axis=1)
+            s = lax.dot_general(qd, kk, (((1,), (1,)), ((), ())), preferred_element_type=F32)
+            ss.append(jnp.where(pos <= len_s[b], s, -jnp.inf))
+        ms = [jnp.maximum(jnp.max(s, axis=-1, keepdims=True), NEG_BIG) for s in ss]
+        ps = [jnp.exp2((s - m) * cs) for s, m in zip(ss, ms)]
+        ls = [jnp.sum(p, axis=-1, keepdims=True) for p in ps]
+        os = []
+        for j, p in zip(js, ps):
+            vv = jnp.concatenate([v_v[j, 0], v_v[j, 1]], axis=1)
+            o2 = jnp.dot(p.astype(BF16), vv, preferred_element_type=F32)
+            os.append(jnp.where(top, o2[:, :HD], o2[:, HD:]))
+        return os, ms, ls
 
     def stats_tile(ms, ls):
         t = jnp.zeros((ROWS, HD), F32)
@@ -146,15 +158,14 @@
             t = jnp.where(lane == 4 + i, ls[i], t)
         return t
 
-    ms, ls = [], []
+    os, ms, ls = attend(range(4))
     for j in range(4):
-        o, m, l = attend(j)
-        ds_b[j] = o
-        ms.append(m)
-        ls.append(l)
+        ds_b[j] = os[j]
     ds_b[4] = stats_tile(ms, ls)
     send(ds_b, dr_b, d_ss.at[0], d_rs.at[0], partner)
-    own = [attend(j) for j in range(4, 8)]
+    cp_wo = start(wo_hbm.at[:, cols], wo_v, w2_sem.at[0])
+    cp_wd = start(wd_hbm.at[:, cols], wd_v, w2_sem.at[1])
+    own = list(zip(*attend(range(4, 8))))
 
     def combine(parts):
         mx = functools.reduce(jnp.maximum, [p[1] for p in parts])
@@ -203,8 +214,8 @@
         recv(mg_b.at[g], mg_ss.at[n], mg_rs.at[g], d)
     ml = jnp.concatenate([mg_b[i % 8, i // 8] for i in range(FF_BLOCKS)], axis=1).astype(BF16)
     cp_wd.wait()
-    r1 = jnp.dot(ml, wd_v[:, :512], preferred_element_type=F32)
-    r2 = jnp.dot(ml, wd_v[:, 512:], preferred_element_type=F32)
+    f_b[:, :512] = jnp.dot(ml, wd_v[:, :512], preferred_element_type=F32)
+    f_b[:, 512:] = jnp.dot(ml, wd_v[:, 512:], preferred_element_type=F32)
 
     for k in (1, 2, 3):
         recv(z_b.at[up(z, k)], z_ss.at[k - 1], z_rs.at[up(z, k)], z_peers[k - 1])
@@ -216,8 +227,8 @@
         of_b[pl.ds(32 + i * 8, 8), :] = o
     ol = jnp.concatenate([of_b[pl.ds(n, 8, stride=8), :] for n in range(8)], axis=1).astype(BF16)
     cp_wo.wait()
-    r1 = r1 + jnp.dot(ol, wo_v[:, :512], preferred_element_type=F32)
-    r2 = r2 + jnp.dot(ol, wo_v[:, 512:], preferred_element_type=F32)
+    r1 = f_b[:, :512] + jnp.dot(ol, wo_v[:, :512], preferred_element_type=F32)
+    r2 = f_b[:, 512:] + jnp.dot(ol, wo_v[:, 512:], preferred_element_type=F32)
 
     upper = lax.broadcasted_iota(jnp.int32, (ROWS, 512), 0) < 4
     keep = jnp.logical_xor(upper, jnp.broadcast_to(c == 1, (ROWS, 512)))
@@ -252,7 +263,7 @@
     def local_step(*args):
         return pl.pallas_call(
             kernel,
-            out_shape=jax.ShapeDtypeStruct((ROWS, HID), BF16),
+            out_shape=pltpu.VMEM((ROWS, HID), BF16),
             in_specs=[any_spec] * 10,
             out_specs=pl.BlockSpec(memory_space=pltpu.VMEM),
             scratch_shapes=[
@@ -274,6 +285,7 @@
                 pltpu.VMEM((4, 5, ROWS, HD), F32),
                 pltpu.VMEM((4, 5, ROWS, HD), F32),
                 pltpu.VMEM((64, HD), F32),
+                pltpu.VMEM((ROWS, 1024), F32),
                 pltpu.VMEM((4, ROWS, 512), F32),
                 pltpu.VMEM((8, ROWS, 512), F32),
                 dma((3,)), dma((WQ_CHUNKS,)), dma((2,)), dma((8,)), dma((8,)), dma((2,)),

time: 38.3 us -> 29.7 us (0.78)
  Pallas kernels: 36.7 us -> 29 us
  local copies, waits for them, and re-layouts: 1.47 us -> 0.63 us
    pallas_call x1, Pallas kernels: 36.7 us -> 29 us  [local_step(): pl.pallas_call(kernel, out_shape=pltpu.VMEM((ROWS, HID), BF16), in_specs=...]
    unnamed x1, local copies, waits for them, and re-layouts: 1.47 us -> 0.63 us
where the time goes in v2:
time: 29.7 us; the launch traced here: 29.6 us
  Pallas kernels  29 us (98%)
  local copies, waits for them, and re-layouts  0.63 us (2%)
    pallas_call x1, Pallas kernels, local_step(): pl.pallas_call(kernel, out_shape=pltpu.VMEM((ROWS, HID), BF16), in_specs=...  29 us
    unnamed x1, local copies, waits for them, and re-layouts  0.63 us

profile of v2, /device:TPU:1, one launch (start us, length us, event | category | flops | bytes accessed | tf_op | source)
XLA Modules:
  0.0 29.6 jit_solution(12372834394146860448)
XLA Ops:
  0.0 29.0 %shard_map.100 = bf16[8,4096]{1,0:T(8,128)(2,1)S(1)} custom-call(bf16[8,4096]{1,0:T(8,128)(2,1)} %x_hbm.1, s32[8]{0:T(128)} %len_hbm.1, bf16[4096]{0:T(1024)(128)(2,1)} %lnw_hbm.1, bf16[4096,1024]{1,0:T(8,128)(2,1)} %wq_hbm.1, bf16[1024,4096]{1,0:T(8,128)(2,1)} %wo_hbm.1, bf16[4096,3584]{1,0:T(8,128)(2,1)} %wg_hbm.1, bf16[4096,3584]{1,0:T(8,128)(2,1)} %wu_hbm.1, ...), custom_call_target="tpu_custom_call" | custom-call | tf_op jit(solution)/shard_map/pallas_call | solution.py:264
  29.0 0.6 %copy.12 = bf16[8,4096]{1,0:T(8,128)(2,1)} copy(bf16[8,4096]{1,0:T(8,128)(2,1)S(1)} %shard_map.100) | data formatting | bytes 131072
